TPU v7x, 128 devices: a whole 4x4x4 slice. The times are simulated.
128 devices in a mesh: row: 2 (over z_lo), col: 64 (over y, x, z_hi, core).
Axes of the slice: x: 4, y: 4, z: 4 (z_hi: 2, z_lo: 2; z = z_hi * 2 + z_lo), core: 2. Of those that a mesh axis runs over, the one named last changes fastest.
Arguments:
- tokens: bfloat16 [512, 4608], P('col', 'row'), may hold values from -6 to 6
- pre_gain: float32 [2, 4608], P(None, 'row'), may hold values from -0.6 to 0.6
- post_gain: float32 [2, 4608], P(None, 'row'), may hold values from -0.6 to 0.6
- gate_weight: bfloat16 [2, 4608, 36864], P(None, ('row', 'col')), may hold values from -0.09375 to 0.09375
- up_weight: bfloat16 [2, 4608, 36864], P(None, ('row', 'col')), may hold values from -0.09375 to 0.09375
- down_weight: bfloat16 [2, 36864, 4608], P(None, ('row', 'col')), may hold values from -0.13541667 to 0.13541667
Outputs:
- stream: bfloat16 [512, 4608], P('col', 'row')
All inputs are finite; a program needn't handle non-finite values.
Results may differ from a plain program's by a relative error of at most 0.019.
Values may be sent and summed in bfloat16 or wider, within the bound.
A program may use at most 128 MiB of HBM per device.

v0:
```python
import jax
import jax.numpy as jnp
from jax import lax
from jax.sharding import Mesh
from jax.sharding import PartitionSpec as P

COL = ("col_0", "col_1", "col_2", "col_3")
ROW_COL = ("row", "col_0", "col_1", "col_2", "col_3")
norm_eps = 1e-06


def sent_to_all(value, axis):
    copies = jnp.broadcast_to(value, (lax.axis_size(axis), *value.shape))
    return lax.all_to_all(copies, axis, split_axis=0, concat_axis=0, tiled=True)


def over_copies(value, axis):
    everything = sent_to_all(value, axis)
    return jnp.sum(everything, axis=0)


def laid_out(blocks, dim):
    lengths = list(blocks.shape[1:])
    lengths[dim] *= blocks.shape[0]
    return jnp.moveaxis(blocks, 0, dim).reshape(lengths)


def whole_of(value, axes, dim):
    far, near = axes
    first = sent_to_all(value, far)
    blocks = jnp.swapaxes(sent_to_all(first, near), 0, 1)
    return laid_out(blocks.reshape(-1, *value.shape), dim)


def over_copies_2(value, axis):
    everything = sent_to_all(value, axis)
    return jnp.sum(everything.astype(jnp.float32), axis=0)


def split_up(value, dim, peers):
    before, after = (value.shape[:dim], value.shape[dim + 1 :])
    return jnp.moveaxis(value.reshape(*before, peers, -1, *after), dim, 0)


def summed_on_arrival(value, axis, dim):
    peers = lax.axis_size(axis)
    blocks = lax.all_to_all(split_up(value, dim, peers), axis, 0, 0, tiled=True)
    return jnp.sum(blocks.astype(jnp.float32), axis=0)


def sum_by_axis(value, axes, dim):
    far, near = axes
    blocks = split_up(value, dim, lax.axis_size(far))
    nearer = summed_on_arrival(blocks, near, dim + 1)
    arrived = lax.all_to_all(
        nearer.astype(jnp.bfloat16), far, split_axis=0, concat_axis=0, tiled=True
    )
    return arrived.astype(jnp.float32).sum(axis=0)


def activate(summed, columns):
    gate = summed[:, :columns]
    up_proj = summed[:, columns:]
    return (jax.nn.gelu(gate, approximate=True) * up_proj).astype(jnp.bfloat16)


def on_device(tokens, pre_gain, post_gain, gate_weight, up_weight, down_weight):
    layer_count = gate_weight.shape[0]
    row_count = lax.axis_size("row")
    col_count = lax.axis_size(COL)
    model_width = tokens.shape[1] * row_count
    stored_rows = gate_weight.shape[1]
    hidden_total = gate_weight.shape[2]
    block_width = hidden_total // (row_count * col_count)
    tile_rows = stored_rows * col_count
    tile_columns = hidden_total // col_count
    gate_split = gate_weight.reshape(layer_count, stored_rows, row_count, col_count, block_width)
    up_split = up_weight.reshape(layer_count, stored_rows, row_count, col_count, block_width)
    gate_tiles, up_tiles = (
        lax.all_to_all(gate_split, COL, split_axis=3, concat_axis=1, tiled=True),
        lax.all_to_all(up_split, COL, split_axis=3, concat_axis=1, tiled=True),
    )
    gate_tiles = gate_tiles.reshape(layer_count, tile_rows, tile_columns)
    up_tiles = up_tiles.reshape(layer_count, tile_rows, tile_columns)
    down_tiles = lax.all_to_all(down_weight, "row", split_axis=2, concat_axis=1, tiled=True)
    current = tokens
    for layer_index in range(layer_count):
        gate_up = jnp.concatenate((gate_tiles[layer_index], up_tiles[layer_index]), axis=1)
        down_tile = down_tiles[layer_index]
        columns = gate_up.shape[1] // 2
        values = current.astype(jnp.float32)
        squares = over_copies(jnp.sum(values * values, axis=1), "row")
        scale_pre = lax.rsqrt(squares / model_width + norm_eps)[:, None]
        normed = (values * scale_pre * (1.0 + pre_gain[layer_index])[None, :]).astype(jnp.bfloat16)
        partial_sums = jnp.dot(
            whole_of(normed, (("col_0", "col_1", "col_2"), "col_3"), 0),
            gate_up,
            preferred_element_type=jnp.float32,
        )
        summed = over_copies_2(partial_sums.astype(jnp.bfloat16), "row").astype(jnp.float32)
        hidden = activate(summed, columns)
        branch = sum_by_axis(
            jnp.dot(hidden, down_tile, preferred_element_type=jnp.float32).astype(jnp.bfloat16),
            (("col_0", "col_1", "col_2"), "col_3"),
            0,
        )
        branch_squares = over_copies(jnp.sum(branch * branch, axis=1), "row")
        scale_post = lax.rsqrt(branch_squares / model_width + norm_eps)[:, None]
        post = branch * scale_post * (1.0 + post_gain[layer_index])[None, :]
        current = (values + post).astype(jnp.bfloat16)
    return current


def solution(mesh):
    split = Mesh(
        mesh.devices.reshape(mesh.shape["row"], 4, 4, 2, 2),
        ("row", "col_0", "col_1", "col_2", "col_3"),
    )
    in_specs = (
        P(COL, "row"),
        P(None, "row"),
        P(None, "row"),
        P(None, ROW_COL, None),
        P(None, ROW_COL, None),
        P(None, ROW_COL, None),
    )
    out_specs = P(COL, "row")
    return jax.shard_map(
        on_device, mesh=split, in_specs=in_specs, out_specs=out_specs, check_vma=False
    )
```

profile of v0, /device:TPU:0, one launch (start us, length us, event | category | flops | bytes accessed | tf_op | source)
XLA Modules:
  0.0 576.6 jit_solution(1357578688195838266)
XLA Ops:
  1.5 3.3 all-to-all-start
  6.2 2.3 all-to-all-done
  10.5 10.6 %all-to-all-start.1 = ((bf16[32,8,2304]{2,1,0:T(8,128)(2,1)}), bf16[32,8,2304]{2,1,0:T(8,128)(2,1)S(1)}, u32[]{:S(2)}, u32[]{:S(2)}) async-start(bf16[32,8,2304]{2,1,0:T(8,128)(2,1)} %broadcast_in_dim.39), calls=%async_computation.1 | async-start | bytes 2359296 | tf_op jit(solution)/shard_map/all_to_all | solution.py:14
  21.1 14.4 %reshape.58 = bf16[2,36,2,64,288]{4,3,2,0,1:T(8,128)(2,1)} reshape(bf16[2,36,36864]{2,0,1:T(2,128)(2,1)} %param.9) | data formatting | bytes 10616832 | tf_op jit(solution)/shard_map/reshape | solution.py:77
  35.5 11.5 %copy.43 = bf16[2,36,2,64,288]{4,2,1,0,3:T(2,128)(2,1)} copy(bf16[2,36,2,64,288]{4,3,2,0,1:T(8,128)(2,1)} %reshape.58) | data formatting | bytes 10616832 | tf_op jit(solution)/shard_map/reshape | solution.py:77
  47.1 5.6 all_to_all.119
  52.7 10.6 %all-to-all-start.3 = ((bf16[2,36,2,64,288]{4,2,1,0,3:T(2,128)(2,1)}), bf16[2,36,2,64,288]{4,2,1,0,3:T(2,128)(2,1)}, u32[]{:S(2)}, u32[]{:S(2)}) async-start(bf16[2,36,2,64,288]{4,2,1,0,3:T(2,128)(2,1)} %copy.43), calls=%async_computation.3 | async-start | bytes 14155776 | tf_op jit(solution)/shard_map/all_to_all | solution.py:80
  63.4 14.4 %reshape.59 = bf16[2,36,2,64,288]{4,3,2,0,1:T(8,128)(2,1)} reshape(bf16[2,36,36864]{2,0,1:T(2,128)(2,1)} %param.10) | data formatting | bytes 10616832 | tf_op jit(solution)/shard_map/reshape | solution.py:78
  77.8 11.5 %copy.44 = bf16[2,36,2,64,288]{4,2,1,0,3:T(2,128)(2,1)} copy(bf16[2,36,2,64,288]{4,3,2,0,1:T(8,128)(2,1)} %reshape.59) | data formatting | bytes 10616832 | tf_op jit(solution)/shard_map/reshape | solution.py:78
  89.3 62.8 %all-to-all-done.3 = bf16[2,36,2,64,288]{4,2,1,0,3:T(2,128)(2,1)} async-done(((bf16[2,36,2,64,288]{4,2,1,0,3:T(2,128)(2,1)}), bf16[2,36,2,64,288]{4,2,1,0,3:T(2,128)(2,1)}, u32[]{:S(2)}, u32[]{:S(2)}) %all-to-all-start.3) | async-done | bytes 5308448 | tf_op jit(solution)/shard_map/all_to_all | solution.py:80
  152.1 16.1 %all-to-all-start.4 = ((bf16[2,36,2,64,288]{4,2,1,0,3:T(2,128)(2,1)}), bf16[2,36,2,64,288]{4,2,1,0,3:T(2,128)(2,1)}, u32[]{:S(2)}, u32[]{:S(2)}) async-start(bf16[2,36,2,64,288]{4,2,1,0,3:T(2,128)(2,1)} %copy.44), calls=%async_computation.4 | async-start | bytes 14155776 | tf_op jit(solution)/shard_map/all_to_all | solution.py:81
  168.1 18.0 %copy.45 = bf16[2,288,4608]{1,0,2:T(2,128)(2,1)} copy(bf16[2,288,4608]{2,1,0:T(8,128)(2,1)} %param.11) | data formatting | bytes 10616832 | tf_op args[5]
  187.7 69.1 %all-to-all-done.4 = bf16[2,36,2,64,288]{4,2,1,0,3:T(2,128)(2,1)} async-done(((bf16[2,36,2,64,288]{4,2,1,0,3:T(2,128)(2,1)}), bf16[2,36,2,64,288]{4,2,1,0,3:T(2,128)(2,1)}, u32[]{:S(2)}, u32[]{:S(2)}) %all-to-all-start.4) | async-done | bytes 5308448 | tf_op jit(solution)/shard_map/all_to_all | solution.py:81
  256.8 6.8 %all-to-all-start.6 = ((bf16[2,288,4608]{1,0,2:T(2,128)(2,1)}), bf16[2,288,4608]{1,0,2:T(2,128)(2,1)}, u32[]{:S(2)}, u32[]{:S(2)}) async-start(bf16[2,288,4608]{1,0,2:T(2,128)(2,1)} %copy.45), calls=%async_computation.6 | async-start | bytes 14155776 | tf_op jit(solution)/shard_map/all_to_all | solution.py:85
  263.7 9.8 %fusion.61 = (bf16[1,64,36,2,1,288]{5,3,2,0,1,4:T(2,128)(2,1)S(1)}, bf16[1,64,36,2,1,288]{5,3,2,0,1,4:T(2,128)(2,1)}) fusion(bf16[2,64,36,2,1,288]{5,3,2,0,1,4:T(2,128)(2,1)} %bitcast.4), kind=kLoop, calls=%fused_computation.80 | loop fusion | bytes 10616832 | tf_op jit(solution)/shard_map/slice | solution.py:88
  273.5 8.5 %squeeze.22 = bf16[2304,576]{1,0:T(8,128)(2,1)} reshape(bf16[1,64,36,2,1,288]{5,3,2,0,1,4:T(2,128)(2,1)} %get-tuple-element.12) | data formatting | bytes 5308416 | tf_op jit(solution)/shard_map/squeeze | solution.py:88
  282.0 10.8 %fusion.62 = (bf16[1,64,36,2,1,288]{5,3,2,0,1,4:T(2,128)(2,1)}, bf16[1,64,36,2,1,288]{5,3,2,0,1,4:T(2,128)(2,1)}) fusion(bf16[2,64,36,2,1,288]{5,3,2,0,1,4:T(2,128)(2,1)} %bitcast.6), kind=kLoop, calls=%fused_computation.81 | loop fusion | bytes 10616832 | tf_op jit(solution)/shard_map/slice | solution.py:88
  292.7 8.0 %squeeze.23 = bf16[2304,576]{1,0:T(8,128)(2,1)} reshape(bf16[1,64,36,2,1,288]{5,3,2,0,1,4:T(2,128)(2,1)} %get-tuple-element.14) | data formatting | bytes 5308416 | tf_op jit(solution)/shard_map/squeeze | solution.py:88
  300.7 7.7 %fusion.11 = bf16[512,1152]{1,0:T(8,128)(2,1)} fusion(bf16[512,2304]{1,0:T(8,128)(2,1)} %bitcast.49, bf16[2304,576]{1,0:T(8,128)(2,1)} %squeeze.23, bf16[2304,576]{1,0:T(8,128)(2,1)} %squeeze.22), kind=kOutput, calls=%fused_computation.13 | convolution fusion | flops 2729115648 | bytes 8847360 | tf_op jit(solution)/shard_map/dot_general | solution.py:95
  308.4 33.6 %all-to-all-done.6 = bf16[2,288,4608]{1,0,2:T(2,128)(2,1)} async-done(((bf16[2,288,4608]{1,0,2:T(2,128)(2,1)}), bf16[2,288,4608]{1,0,2:T(2,128)(2,1)}, u32[]{:S(2)}, u32[]{:S(2)}) %all-to-all-start.6) | async-done | bytes 5308448 | tf_op jit(solution)/shard_map/all_to_all | solution.py:85
  342.0 2.8 broadcast_in_dim.41
  344.8 4.9 all-to-all-start.5
  349.8 33.0 %copy.55 = bf16[2,288,2,2304]{3,2,1,0:T(2,128)(2,1)} copy(bf16[2,288,2,2304]{1,0,3,2:T(2,128)(2,1)} %bitcast.7) | data formatting | bytes 10616832 | tf_op jit(solution)/shard_map/all_to_all | solution.py:85
  382.8 7.0 %fusion.63 = (bf16[1,2,288,2304]{3,1,2,0:T(2,128)(2,1)}, bf16[1,2,288,2304]{3,1,2,0:T(2,128)(2,1)S(1)}) fusion(bf16[2,2,288,2304]{3,1,2,0:T(2,128)(2,1)} %bitcast.44), kind=kLoop, calls=%fused_computation.82 | loop fusion | bytes 10616832 | tf_op jit(solution)/shard_map/slice | solution.py:89
  389.8 1.8 copy.47
  391.6 2.5 convert_reduce_fusion.1
  394.1 2.3 convolution_convert_fusion.1
  396.6 6.5 %all_to_all.120 = bf16[2,32,8,2304]{3,2,1,0:T(8,128)(2,1)} all-to-all(bf16[2,32,8,2304]{3,2,1,0:T(8,128)(2,1)S(1)} %bitcast.45), channel_id=1, replica_groups=mesh['row'=2,'col_0'=4,'col_1'=4,'col_2'=2,'col_3'=2] {'col_3'}, dimensions={0} | all-to-all | bytes 4718592 | tf_op jit(solution)/shard_map/all_to_all | solution.py:47
  403.1 3.4 reduce_sum.135
  406.6 15.8 %all-to-all-start.8 = ((bf16[32,8,2304]{2,1,0:T(8,128)(2,1)}), bf16[32,8,2304]{2,1,0:T(8,128)(2,1)}, u32[]{:S(2)}, u32[]{:S(2)}) async-start(bf16[32,8,2304]{2,1,0:T(8,128)(2,1)} %reduce_sum.135), calls=%async_computation.8 | async-start | bytes 2359296 | tf_op jit(solution)/shard_map/all_to_all | solution.py:55
  423.8 19.6 %all-to-all-done.8 = bf16[32,8,2304]{2,1,0:T(8,128)(2,1)} async-done(((bf16[32,8,2304]{2,1,0:T(8,128)(2,1)}), bf16[32,8,2304]{2,1,0:T(8,128)(2,1)}, u32[]{:S(2)}, u32[]{:S(2)}) %all-to-all-start.8) | async-done | bytes 1179680 | tf_op jit(solution)/shard_map/all_to_all | solution.py:55
  445.6 6.2 %all_to_all.121 = f32[2,1,8]{2,1,0:T(1,128)S(1)} all-to-all(f32[2,1,8]{2,1,0:T(1,128)S(1)} %broadcast_in_dim.42), channel_id=1, replica_groups=mesh['row'=2,'col_0'=4,'col_1'=4,'col_2'=2,'col_3'=2] {'row'}, dimensions={0} | all-to-all | bytes 128 | tf_op jit(solution)/shard_map/all_to_all | solution.py:14
  453.0 1.7 fusion.46
  454.7 6.1 %all_to_all.122 = f32[2,1,8]{2,1,0:T(1,128)S(1)} all-to-all(f32[2,1,8]{2,1,0:T(1,128)S(1)} %broadcast_in_dim.43), channel_id=1, replica_groups=mesh['row'=2,'col_0'=4,'col_1'=4,'col_2'=2,'col_3'=2] {'row'}, dimensions={0} | all-to-all | bytes 128 | tf_op jit(solution)/shard_map/all_to_all | solution.py:14
  464.0 4.7 all-to-all-start.11
  468.7 4.0 squeeze.25
  472.8 6.9 %squeeze.26 = bf16[2304,576]{1,0:T(8,128)(2,1)S(1)} reshape(bf16[1,64,36,2,1,288]{5,3,2,0,1,4:T(2,128)(2,1)} %get-tuple-element.13) | data formatting | bytes 5308416 | tf_op jit(solution)/shard_map/squeeze | solution.py:88
  479.7 6.5 %all-to-all-done.11 = bf16[32,8,2304]{2,1,0:T(8,128)(2,1)} async-done(((bf16[32,8,2304]{2,1,0:T(8,128)(2,1)}), bf16[32,8,2304]{2,1,0:T(8,128)(2,1)}, u32[]{:S(2)}, u32[]{:S(2)}) %all-to-all-start.11) | async-done | bytes 1179680 | tf_op jit(solution)/shard_map/all_to_all | solution.py:14
  487.6 5.6 all_to_all.123
  495.1 3.2 fusion.8
  500.0 5.4 all-to-all-start.13
  505.4 1.8 copy.52
  507.2 26.5 %all-to-all-done.13 = bf16[2,512,1152]{2,1,0:T(8,128)(2,1)} async-done(((bf16[2,512,1152]{2,1,0:T(8,128)(2,1)}), bf16[2,512,1152]{2,1,0:T(8,128)(2,1)}, u32[]{:S(2)}, u32[]{:S(2)}) %all-to-all-start.13) | async-done | bytes 2359328 | tf_op jit(solution)/shard_map/all_to_all | solution.py:14
  533.7 2.4 convert_reduce_fusion
  536.1 2.3 convolution_convert_fusion
  538.6 5.6 all_to_all.124
  544.8 24.4 %all_to_all.125 = bf16[32,8,2304]{2,1,0:T(8,128)(2,1)S(1)} all-to-all(bf16[32,8,2304]{2,1,0:T(8,128)(2,1)S(1)} %reduce_sum.142), channel_id=1, replica_groups=mesh['row'=2,'col_0'=4,'col_1'=4,'col_2'=2,'col_3'=2] {'col_0','col_1','..., dimensions={0} | all-to-all | bytes 2359296 | tf_op jit(solution)/shard_map/all_to_all | solution.py:55
  569.6 6.1 %all_to_all.126 = f32[2,1,8]{2,1,0:T(1,128)S(1)} all-to-all(f32[2,1,8]{2,1,0:T(1,128)S(1)} %broadcast_in_dim.47), channel_id=1, replica_groups=mesh['row'=2,'col_0'=4,'col_1'=4,'col_2'=2,'col_3'=2] {'row'}, dimensions={0} | all-to-all | bytes 128 | tf_op jit(solution)/shard_map/all_to_all | solution.py:14
  (46 shorter events, 21.6 us)
Async XLA Ops:
  1.5 7.0 %all-to-all-start = ((f32[2,1,8]{2,1,0:T(1,128)}), f32[2,1,8]{2,1,0:T(1,128)S(1)}, u32[]{:S(2)}, u32[]{:S(2)}) async-start(f32[2,1,8]{2,1,0:T(1,128)} %broadcast_in_dim.38), calls=%async_computation | async-start | bytes 2048 | tf_op jit(solution)/shard_map/all_to_all | solution.py:14
  10.5 36.5 %all-to-all-start.1 = ((bf16[32,8,2304]{2,1,0:T(8,128)(2,1)}), bf16[32,8,2304]{2,1,0:T(8,128)(2,1)S(1)}, u32[]{:S(2)}, u32[]{:S(2)}) async-start(bf16[32,8,2304]{2,1,0:T(8,128)(2,1)} %broadcast_in_dim.39), calls=%async_computation.1 | async-start | bytes 2359296 | tf_op jit(solution)/shard_map/all_to_all | solution.py:14
  52.7 99.3 %all-to-all-start.3 = ((bf16[2,36,2,64,288]{4,2,1,0,3:T(2,128)(2,1)}), bf16[2,36,2,64,288]{4,2,1,0,3:T(2,128)(2,1)}, u32[]{:S(2)}, u32[]{:S(2)}) async-start(bf16[2,36,2,64,288]{4,2,1,0,3:T(2,128)(2,1)} %copy.43), calls=%async_computation.3 | async-start | bytes 14155776 | tf_op jit(solution)/shard_map/all_to_all | solution.py:80
  152.1 104.7 %all-to-all-start.4 = ((bf16[2,36,2,64,288]{4,2,1,0,3:T(2,128)(2,1)}), bf16[2,36,2,64,288]{4,2,1,0,3:T(2,128)(2,1)}, u32[]{:S(2)}, u32[]{:S(2)}) async-start(bf16[2,36,2,64,288]{4,2,1,0,3:T(2,128)(2,1)} %copy.44), calls=%async_computation.4 | async-start | bytes 14155776 | tf_op jit(solution)/shard_map/all_to_all | solution.py:81
  256.8 85.1 %all-to-all-start.6 = ((bf16[2,288,4608]{1,0,2:T(2,128)(2,1)}), bf16[2,288,4608]{1,0,2:T(2,128)(2,1)}, u32[]{:S(2)}, u32[]{:S(2)}) async-start(bf16[2,288,4608]{1,0,2:T(2,128)(2,1)} %copy.45), calls=%async_computation.6 | async-start | bytes 14155776 | tf_op jit(solution)/shard_map/all_to_all | solution.py:85
  344.8 46.8 %all-to-all-start.5 = ((bf16[2,512,1152]{2,1,0:T(8,128)(2,1)}), bf16[2,512,1152]{2,1,0:T(8,128)(2,1)}, u32[]{:S(2)}, u32[]{:S(2)}) async-start(bf16[2,512,1152]{2,1,0:T(8,128)(2,1)} %broadcast_in_dim.41), calls=%async_computation.5 | async-start | bytes 4718592 | tf_op jit(solution)/shard_map/all_to_all | solution.py:14
  391.6 2.5 copy-start.2
  406.6 36.9 %all-to-all-start.8 = ((bf16[32,8,2304]{2,1,0:T(8,128)(2,1)}), bf16[32,8,2304]{2,1,0:T(8,128)(2,1)}, u32[]{:S(2)}, u32[]{:S(2)}) async-start(bf16[32,8,2304]{2,1,0:T(8,128)(2,1)} %reduce_sum.135), calls=%async_computation.8 | async-start | bytes 2359296 | tf_op jit(solution)/shard_map/all_to_all | solution.py:55
  444.9 0.6 copy-start.4
  464.0 22.1 %all-to-all-start.11 = ((bf16[32,8,2304]{2,1,0:T(8,128)(2,1)}), bf16[32,8,2304]{2,1,0:T(8,128)(2,1)}, u32[]{:S(2)}, u32[]{:S(2)}) async-start(bf16[32,8,2304]{2,1,0:T(8,128)(2,1)} %broadcast_in_dim.44), calls=%async_computation.11 | async-start | bytes 2359296 | tf_op jit(solution)/shard_map/all_to_all | solution.py:14
  493.3 1.8 copy-start.1
  500.0 5.4 copy-start
  500.0 33.7 %all-to-all-start.13 = ((bf16[2,512,1152]{2,1,0:T(8,128)(2,1)}), bf16[2,512,1152]{2,1,0:T(8,128)(2,1)}, u32[]{:S(2)}, u32[]{:S(2)}) async-start(bf16[2,512,1152]{2,1,0:T(8,128)(2,1)} %broadcast_in_dim.46), calls=%async_computation.13 | async-start | bytes 4718592 | tf_op jit(solution)/shard_map/all_to_all | solution.py:14
  507.2 28.9 %copy-start.3 = (bf16[1,2,288,2304]{3,2,1,0:T(8,128)(2,1)S(1)}, bf16[1,2,288,2304]{3,2,1,0:T(8,128)(2,1)}, u32[]{:S(2)}) copy-start(bf16[1,2,288,2304]{3,2,1,0:T(8,128)(2,1)} %copy.52) | copy-start | bytes 7962628
  544.8 30.9 %copy-start.5 = (bf16[8,2304]{1,0:T(8,128)(2,1)S(1)}, bf16[8,2304]{1,0:T(8,128)(2,1)}, u32[]{:S(2)}) copy-start(bf16[8,2304]{1,0:T(8,128)(2,1)} %get-tuple-element.10) | copy-start | bytes 110596
where the time goes:
time: 586 us; the launch traced here: 577 us
  waiting for transfers between devices  220 us (38%)
  local copies, waits for them, and re-layouts  175 us (30%)
  starting transfers between devices  78.3 us (13%)
  blocking collectives  66.3 us (11%)
  other arithmetic  21.2 us (4%)
  matrix products  15.6 us (3%)
    all_to_all x1, waiting for transfers between devices, on_device(): lax.all_to_all(up_split, COL, split_axis=3, concat_axis=1, tiled=True)  69.1 us
    all_to_all x1, waiting for transfers between devices, on_device(): lax.all_to_all(gate_split, COL, split_axis=3, concat_axis=1, tiled=True)  62.8 us
    all_to_all x5, waiting for transfers between devices, sent_to_all(): return lax.all_to_all(copies, axis, split_axis=0, concat_axis=0, tiled=True)  35.2 us
    all_to_all x1, waiting for transfers between devices, on_device(): lax.all_to_all(down_weight, 'row', split_axis=2, concat_axis=1, tiled=True)  33.6 us
    all_to_all x1, local copies, waits for them, and re-layouts, on_device(): lax.all_to_all(down_weight, 'row', split_axis=2, concat_axis=1, tiled=True)  33 us
    all_to_all x5, blocking collectives, sent_to_all(): return lax.all_to_all(copies, axis, split_axis=0, concat_axis=0, tiled=True)  29.7 us
    all_to_all x5, starting transfers between devices, sent_to_all(): return lax.all_to_all(copies, axis, split_axis=0, concat_axis=0, tiled=True)  28.9 us
    reshape x2, local copies, waits for them, and re-layouts, on_device(): up_weight.reshape(layer_count, stored_rows, row_count, col_count, block_w...  25.9 us
  transfers between devices with their start and end apart: 9, of which 7 were waited for; matrix products, arithmetic and copies ran while one was open for 30% of the time, Pallas kernels for 0%

commit v1 on v0

--- a/solution.py
+++ b/solution.py
@@ -82,7 +82,10 @@
     )
     gate_tiles = gate_tiles.reshape(layer_count, tile_rows, tile_columns)
     up_tiles = up_tiles.reshape(layer_count, tile_rows, tile_columns)
-    down_tiles = lax.all_to_all(down_weight, "row", split_axis=2, concat_axis=1, tiled=True)
+    size = lax.axis_size("row")
+    shards = jnp.stack(jnp.split(down_weight, size, axis=2), axis=0)
+    shards = lax.all_to_all(shards, "row", split_axis=0, concat_axis=0)
+    down_tiles = jnp.concatenate(shards, axis=1)
     current = tokens
     for layer_index in range(layer_count):
         gate_up = jnp.concatenate((gate_tiles[layer_index], up_tiles[layer_index]), axis=1)

time: 586 us -> 547 us (0.933)
  local copies, waits for them, and re-layouts: 175 us -> 121 us
  blocking collectives: 66.3 us -> 97.1 us
  waiting for transfers between devices: 220 us -> 209 us
    all_to_all x1 -> x0, local copies, waits for them, and re-layouts: 33 us -> none  [on_device(): lax.all_to_all(down_weight, 'row', split_axis=2, concat_axis=1, tiled=True)]
    all_to_all x5 -> x6, blocking collectives: 29.7 us -> 60.5 us  [sent_to_all(): return lax.all_to_all(copies, axis, split_axis=0, concat_axis=0, tiled=True)]
    all_to_all x1, waiting for transfers between devices: 33.6 us -> 14.6 us  [on_device(): shards = lax.all_to_all(shards, 'row', split_axis=0, concat_axis=0)]
    unnamed x13 -> x10, local copies, waits for them, and re-layouts: 20.3 us -> 3.63 us
    all_to_all x1, waiting for transfers between devices: 69.1 us -> 81.4 us  [on_device(): lax.all_to_all(up_split, COL, split_axis=3, concat_axis=1, tiled=True)]
    all_to_all x5 -> x4, starting transfers between devices: 28.9 us -> 23.7 us  [sent_to_all(): return lax.all_to_all(copies, axis, split_axis=0, concat_axis=0, tiled=True)]
    all_to_all x5 -> x4, waiting for transfers between devices: 35.2 us -> 30.5 us  [sent_to_all(): return lax.all_to_all(copies, axis, split_axis=0, concat_axis=0, tiled=True)]
  transfers between devices with their start and end apart: 9 -> 8, of which waited for: 7 -> 7; matrix products, arithmetic and copies ran while one was open for 30% -> 23% of each run, Pallas kernels for 0% -> 0%
where the time goes in v1:
time: 547 us; the launch traced here: 538 us
  waiting for transfers between devices  209 us (38%)
  local copies, waits for them, and re-layouts  121 us (22%)
  blocking collectives  97.1 us (18%)
  starting transfers between devices  73 us (13%)
  other arithmetic  21.9 us (4%)
  matrix products  15.6 us (3%)
    all_to_all x1, waiting for transfers between devices, on_device(): lax.all_to_all(up_split, COL, split_axis=3, concat_axis=1, tiled=True)  81.4 us
    all_to_all x1, waiting for transfers between devices, on_device(): lax.all_to_all(gate_split, COL, split_axis=3, concat_axis=1, tiled=True)  62.8 us
    all_to_all x6, blocking collectives, sent_to_all(): return lax.all_to_all(copies, axis, split_axis=0, concat_axis=0, tiled=True)  60.5 us
    all_to_all x4, waiting for transfers between devices, sent_to_all(): return lax.all_to_all(copies, axis, split_axis=0, concat_axis=0, tiled=True)  30.5 us
    reshape x2, local copies, waits for them, and re-layouts, on_device(): up_weight.reshape(layer_count, stored_rows, row_count, col_count, block_w...  25.9 us
    reshape x2, local copies, waits for them, and re-layouts, on_device(): gate_weight.reshape(layer_count, stored_rows, row_count, col_count, block...  25.9 us
    all_to_all x1, blocking collectives, sum_by_axis(): lax.all_to_all(nearer.astype(jnp.bfloat16), far, split_axis=0, concat_axi...  24.4 us
    all_to_all x4, starting transfers between devices, sent_to_all(): return lax.all_to_all(copies, axis, split_axis=0, concat_axis=0, tiled=True)  23.7 us
  transfers between devices with their start and end apart: 8, of which 7 were waited for; matrix products, arithmetic and copies ran while one was open for 23% of the time, Pallas kernels for 0%

profile of v1, /device:TPU:0, one launch (start us, length us, event | category | flops | bytes accessed | tf_op | source)
XLA Modules:
  0.0 537.9 jit_solution(2821316158094079224)
XLA Ops:
  1.5 3.3 all-to-all-start
  6.2 2.3 all-to-all-done
  10.5 10.6 %all-to-all-start.1 = ((bf16[32,8,2304]{2,1,0:T(8,128)(2,1)}), bf16[32,8,2304]{2,1,0:T(8,128)(2,1)S(1)}, u32[]{:S(2)}, u32[]{:S(2)}) async-start(bf16[32,8,2304]{2,1,0:T(8,128)(2,1)} %broadcast_in_dim.39), calls=%async_computation.1 | async-start | bytes 2359296 | tf_op jit(solution)/shard_map/all_to_all | solution.py:14
  21.1 14.4 %reshape.62 = bf16[2,36,2,64,288]{4,3,2,0,1:T(8,128)(2,1)} reshape(bf16[2,36,36864]{2,0,1:T(2,128)(2,1)} %param.9) | data formatting | bytes 10616832 | tf_op jit(solution)/shard_map/reshape | solution.py:77
  35.5 11.4 %copy.27 = bf16[2,36,2,64,288]{4,2,1,0,3:T(2,128)(2,1)} copy(bf16[2,36,2,64,288]{4,3,2,0,1:T(8,128)(2,1)} %reshape.62) | data formatting | bytes 10616832 | tf_op jit(solution)/shard_map/reshape | solution.py:77
  47.1 5.6 %all_to_all.109 = bf16[2,32,8,2304]{3,2,1,0:T(8,128)(2,1)S(1)} all-to-all(bf16[2,32,8,2304]{3,2,1,0:T(8,128)(2,1)S(1)} %broadcast_in_dim.40), channel_id=1, replica_groups=mesh['row'=2,'col_0'=4,'col_1'=4,'col_2'=2,'col_3'=2] {'col_3'}, dimensions={0} | all-to-all | bytes 4718592 | tf_op jit(solution)/shard_map/all_to_all | solution.py:14
  52.8 10.6 %all-to-all-start.3 = ((bf16[2,36,2,64,288]{4,2,1,0,3:T(2,128)(2,1)}), bf16[2,36,2,64,288]{4,2,1,0,3:T(2,128)(2,1)}, u32[]{:S(2)}, u32[]{:S(2)}) async-start(bf16[2,36,2,64,288]{4,2,1,0,3:T(2,128)(2,1)} %copy.27), calls=%async_computation.3 | async-start | bytes 14155776 | tf_op jit(solution)/shard_map/all_to_all | solution.py:80
  63.4 14.4 %reshape.63 = bf16[2,36,2,64,288]{4,3,2,0,1:T(8,128)(2,1)} reshape(bf16[2,36,36864]{2,0,1:T(2,128)(2,1)} %param.10) | data formatting | bytes 10616832 | tf_op jit(solution)/shard_map/reshape | solution.py:78
  77.8 11.5 %copy.28 = bf16[2,36,2,64,288]{4,2,1,0,3:T(2,128)(2,1)} copy(bf16[2,36,2,64,288]{4,3,2,0,1:T(8,128)(2,1)} %reshape.63) | data formatting | bytes 10616832 | tf_op jit(solution)/shard_map/reshape | solution.py:78
  89.3 62.8 %all-to-all-done.3 = bf16[2,36,2,64,288]{4,2,1,0,3:T(2,128)(2,1)} async-done(((bf16[2,36,2,64,288]{4,2,1,0,3:T(2,128)(2,1)}), bf16[2,36,2,64,288]{4,2,1,0,3:T(2,128)(2,1)}, u32[]{:S(2)}, u32[]{:S(2)}) %all-to-all-start.3) | async-done | bytes 5308448 | tf_op jit(solution)/shard_map/all_to_all | solution.py:80
  152.1 16.1 %all-to-all-start.4 = ((bf16[2,36,2,64,288]{4,2,1,0,3:T(2,128)(2,1)}), bf16[2,36,2,64,288]{4,2,1,0,3:T(2,128)(2,1)}, u32[]{:S(2)}, u32[]{:S(2)}) async-start(bf16[2,36,2,64,288]{4,2,1,0,3:T(2,128)(2,1)} %copy.28), calls=%async_computation.4 | async-start | bytes 14155776 | tf_op jit(solution)/shard_map/all_to_all | solution.py:81
  168.2 2.9 slice_bitcast_fusion.1
  171.1 2.8 pad_maximum_fusion
  173.9 1.5 copy.26
  175.4 81.4 %all-to-all-done.4 = bf16[2,36,2,64,288]{4,2,1,0,3:T(2,128)(2,1)} async-done(((bf16[2,36,2,64,288]{4,2,1,0,3:T(2,128)(2,1)}), bf16[2,36,2,64,288]{4,2,1,0,3:T(2,128)(2,1)}, u32[]{:S(2)}, u32[]{:S(2)}) %all-to-all-start.4) | async-done | bytes 5308448 | tf_op jit(solution)/shard_map/all_to_all | solution.py:81
  256.8 6.2 %all-to-all-start.6 = ((bf16[2,2,288,2304]{3,2,1,0:T(8,128)(2,1)}), bf16[2,2,288,2304]{3,2,1,0:T(8,128)(2,1)}, u32[]{:S(2)}, u32[]{:S(2)}) async-start(bf16[2,2,288,2304]{3,2,1,0:T(8,128)(2,1)} %pad_maximum_fusion), calls=%async_computation.6 | async-start | bytes 10616832 | tf_op jit(solution)/shard_map/all_to_all | solution.py:87
  263.1 9.8 %fusion.61 = (bf16[1,64,36,2,1,288]{5,3,2,0,1,4:T(2,128)(2,1)S(1)}, bf16[1,64,36,2,1,288]{5,3,2,0,1,4:T(2,128)(2,1)}) fusion(bf16[2,64,36,2,1,288]{5,3,2,0,1,4:T(2,128)(2,1)} %bitcast.4), kind=kLoop, calls=%fused_computation.83 | loop fusion | bytes 10616832 | tf_op jit(solution)/shard_map/slice | solution.py:91
  272.9 8.4 %squeeze.22 = bf16[2304,576]{1,0:T(8,128)(2,1)} reshape(bf16[1,64,36,2,1,288]{5,3,2,0,1,4:T(2,128)(2,1)} %get-tuple-element.12) | data formatting | bytes 5308416 | tf_op jit(solution)/shard_map/squeeze | solution.py:91
  281.3 10.9 %fusion.62 = (bf16[1,64,36,2,1,288]{5,3,2,0,1,4:T(2,128)(2,1)}, bf16[1,64,36,2,1,288]{5,3,2,0,1,4:T(2,128)(2,1)}) fusion(bf16[2,64,36,2,1,288]{5,3,2,0,1,4:T(2,128)(2,1)} %bitcast.6), kind=kLoop, calls=%fused_computation.84 | loop fusion | bytes 10616832 | tf_op jit(solution)/shard_map/slice | solution.py:91
  292.2 8.0 %squeeze.23 = bf16[2304,576]{1,0:T(8,128)(2,1)} reshape(bf16[1,64,36,2,1,288]{5,3,2,0,1,4:T(2,128)(2,1)} %get-tuple-element.14) | data formatting | bytes 5308416 | tf_op jit(solution)/shard_map/squeeze | solution.py:91
  300.1 7.7 %fusion.11 = bf16[512,1152]{1,0:T(8,128)(2,1)} fusion(bf16[512,2304]{1,0:T(8,128)(2,1)} %bitcast.51, bf16[2304,576]{1,0:T(8,128)(2,1)} %squeeze.23, bf16[2304,576]{1,0:T(8,128)(2,1)} %squeeze.22), kind=kOutput, calls=%fused_computation.14 | convolution fusion | flops 2729115648 | bytes 8847360 | tf_op jit(solution)/shard_map/dot_general | solution.py:98
  307.8 14.6 %all-to-all-done.6 = bf16[2,2,288,2304]{3,2,1,0:T(8,128)(2,1)} async-done(((bf16[2,2,288,2304]{3,2,1,0:T(8,128)(2,1)}), bf16[2,2,288,2304]{3,2,1,0:T(8,128)(2,1)}, u32[]{:S(2)}, u32[]{:S(2)}) %all-to-all-start.6) | async-done | bytes 5308448 | tf_op jit(solution)/shard_map/all_to_all | solution.py:87
  322.4 2.9 broadcast_in_dim.41
  325.3 5.1 all-to-all-start.5
  330.4 5.3 fusion.63
  335.7 21.6 %all-to-all-done.5 = bf16[2,512,1152]{2,1,0:T(8,128)(2,1)} async-done(((bf16[2,512,1152]{2,1,0:T(8,128)(2,1)}), bf16[2,512,1152]{2,1,0:T(8,128)(2,1)}, u32[]{:S(2)}, u32[]{:S(2)}) %all-to-all-start.5) | async-done | bytes 2359328 | tf_op jit(solution)/shard_map/all_to_all | solution.py:14
  357.3 2.5 convert_reduce_fusion.1
  359.8 2.3 convolution_convert_fusion.1
  362.3 6.5 %all_to_all.110 = bf16[2,32,8,2304]{3,2,1,0:T(8,128)(2,1)} all-to-all(bf16[2,32,8,2304]{3,2,1,0:T(8,128)(2,1)S(1)} %bitcast.47), channel_id=1, replica_groups=mesh['row'=2,'col_0'=4,'col_1'=4,'col_2'=2,'col_3'=2] {'col_3'}, dimensions={0} | all-to-all | bytes 4718592 | tf_op jit(solution)/shard_map/all_to_all | solution.py:47
  368.8 3.4 reduce_sum.135
  372.2 16.3 %all-to-all-start.8 = ((bf16[32,8,2304]{2,1,0:T(8,128)(2,1)}), bf16[32,8,2304]{2,1,0:T(8,128)(2,1)}, u32[]{:S(2)}, u32[]{:S(2)}) async-start(bf16[32,8,2304]{2,1,0:T(8,128)(2,1)} %reduce_sum.135), calls=%async_computation.8 | async-start | bytes 2359296 | tf_op jit(solution)/shard_map/all_to_all | solution.py:55
  388.6 1.5 add_reduce_fusion
  390.0 19.6 %all-to-all-done.8 = bf16[32,8,2304]{2,1,0:T(8,128)(2,1)} async-done(((bf16[32,8,2304]{2,1,0:T(8,128)(2,1)}), bf16[32,8,2304]{2,1,0:T(8,128)(2,1)}, u32[]{:S(2)}, u32[]{:S(2)}) %all-to-all-start.8) | async-done | bytes 1179680 | tf_op jit(solution)/shard_map/all_to_all | solution.py:55
  411.8 6.1 %all_to_all.111 = f32[2,1,8]{2,1,0:T(1,128)S(1)} all-to-all(f32[2,1,8]{2,1,0:T(1,128)S(1)} %broadcast_in_dim.42), channel_id=1, replica_groups=mesh['row'=2,'col_0'=4,'col_1'=4,'col_2'=2,'col_3'=2] {'row'}, dimensions={0} | all-to-all | bytes 128 | tf_op jit(solution)/shard_map/all_to_all | solution.py:14
  419.1 1.7 fusion.46
  420.8 6.1 %all_to_all.112 = f32[2,1,8]{2,1,0:T(1,128)S(1)} all-to-all(f32[2,1,8]{2,1,0:T(1,128)S(1)} %broadcast_in_dim.43), channel_id=1, replica_groups=mesh['row'=2,'col_0'=4,'col_1'=4,'col_2'=2,'col_3'=2] {'row'}, dimensions={0} | all-to-all | bytes 128 | tf_op jit(solution)/shard_map/all_to_all | solution.py:14
  430.0 4.7 all-to-all-start.11
  434.7 4.0 squeeze.25
  438.7 6.9 %squeeze.26 = bf16[2304,576]{1,0:T(8,128)(2,1)S(1)} reshape(bf16[1,64,36,2,1,288]{5,3,2,0,1,4:T(2,128)(2,1)} %get-tuple-element.13) | data formatting | bytes 5308416 | tf_op jit(solution)/shard_map/squeeze | solution.py:91
  445.6 6.6 %all-to-all-done.11 = bf16[32,8,2304]{2,1,0:T(8,128)(2,1)} async-done(((bf16[32,8,2304]{2,1,0:T(8,128)(2,1)}), bf16[32,8,2304]{2,1,0:T(8,128)(2,1)}, u32[]{:S(2)}, u32[]{:S(2)}) %all-to-all-start.11) | async-done | bytes 1179680 | tf_op jit(solution)/shard_map/all_to_all | solution.py:14
  453.7 5.6 %all_to_all.113 = bf16[2,32,8,2304]{3,2,1,0:T(8,128)(2,1)S(1)} all-to-all(bf16[2,32,8,2304]{3,2,1,0:T(8,128)(2,1)S(1)} %broadcast_in_dim.45), channel_id=1, replica_groups=mesh['row'=2,'col_0'=4,'col_1'=4,'col_2'=2,'col_3'=2] {'col_3'}, dimensions={0} | all-to-all | bytes 4718592 | tf_op jit(solution)/shard_map/all_to_all | solution.py:14
  459.5 1.7 copy-done
  461.1 3.2 fusion.8
  464.6 31.0 %all_to_all.114 = bf16[2,512,1152]{2,1,0:T(8,128)(2,1)S(1)} all-to-all(bf16[2,512,1152]{2,1,0:T(8,128)(2,1)S(1)} %broadcast_in_dim.46), channel_id=1, replica_groups=mesh['row'=2,'col_0'=4,'col_1'=4,'col_2'=2,'col_3'=2] {'row'}, dimensions={0} | all-to-all | bytes 4718592 | tf_op jit(solution)/shard_map/all_to_all | solution.py:14
  497.3 2.3 convolution_convert_fusion
  499.8 5.6 %all_to_all.115 = bf16[2,32,8,2304]{3,2,1,0:T(8,128)(2,1)S(1)} all-to-all(bf16[2,32,8,2304]{3,2,1,0:T(8,128)(2,1)S(1)} %bitcast.48), channel_id=1, replica_groups=mesh['row'=2,'col_0'=4,'col_1'=4,'col_2'=2,'col_3'=2] {'col_3'}, dimensions={0} | all-to-all | bytes 4718592 | tf_op jit(solution)/shard_map/all_to_all | solution.py:47
  506.1 24.4 %all_to_all.116 = bf16[32,8,2304]{2,1,0:T(8,128)(2,1)S(1)} all-to-all(bf16[32,8,2304]{2,1,0:T(8,128)(2,1)S(1)} %reduce_sum.142), channel_id=1, replica_groups=mesh['row'=2,'col_0'=4,'col_1'=4,'col_2'=2,'col_3'=2] {'col_0','col_1','..., dimensions={0} | all-to-all | bytes 2359296 | tf_op jit(solution)/shard_map/all_to_all | solution.py:55
  530.8 6.1 %all_to_all.117 = f32[2,1,8]{2,1,0:T(1,128)S(1)} all-to-all(f32[2,1,8]{2,1,0:T(1,128)S(1)} %broadcast_in_dim.47), channel_id=1, replica_groups=mesh['row'=2,'col_0'=4,'col_1'=4,'col_2'=2,'col_3'=2] {'row'}, dimensions={0} | all-to-all | bytes 128 | tf_op jit(solution)/shard_map/all_to_all | solution.py:14
  (41 shorter events, 17.0 us)
Async XLA Ops:
  1.5 7.0 %all-to-all-start = ((f32[2,1,8]{2,1,0:T(1,128)}), f32[2,1,8]{2,1,0:T(1,128)S(1)}, u32[]{:S(2)}, u32[]{:S(2)}) async-start(f32[2,1,8]{2,1,0:T(1,128)} %broadcast_in_dim.38), calls=%async_computation | async-start | bytes 2048 | tf_op jit(solution)/shard_map/all_to_all | solution.py:14
  10.5 36.5 %all-to-all-start.1 = ((bf16[32,8,2304]{2,1,0:T(8,128)(2,1)}), bf16[32,8,2304]{2,1,0:T(8,128)(2,1)S(1)}, u32[]{:S(2)}, u32[]{:S(2)}) async-start(bf16[32,8,2304]{2,1,0:T(8,128)(2,1)} %broadcast_in_dim.39), calls=%async_computation.1 | async-start | bytes 2359296 | tf_op jit(solution)/shard_map/all_to_all | solution.py:14
  52.8 99.3 %all-to-all-start.3 = ((bf16[2,36,2,64,288]{4,2,1,0,3:T(2,128)(2,1)}), bf16[2,36,2,64,288]{4,2,1,0,3:T(2,128)(2,1)}, u32[]{:S(2)}, u32[]{:S(2)}) async-start(bf16[2,36,2,64,288]{4,2,1,0,3:T(2,128)(2,1)} %copy.27), calls=%async_computation.3 | async-start | bytes 14155776 | tf_op jit(solution)/shard_map/all_to_all | solution.py:80
  152.1 104.7 %all-to-all-start.4 = ((bf16[2,36,2,64,288]{4,2,1,0,3:T(2,128)(2,1)}), bf16[2,36,2,64,288]{4,2,1,0,3:T(2,128)(2,1)}, u32[]{:S(2)}, u32[]{:S(2)}) async-start(bf16[2,36,2,64,288]{4,2,1,0,3:T(2,128)(2,1)} %copy.28), calls=%async_computation.4 | async-start | bytes 14155776 | tf_op jit(solution)/shard_map/all_to_all | solution.py:81
  256.8 65.6 %all-to-all-start.6 = ((bf16[2,2,288,2304]{3,2,1,0:T(8,128)(2,1)}), bf16[2,2,288,2304]{3,2,1,0:T(8,128)(2,1)}, u32[]{:S(2)}, u32[]{:S(2)}) async-start(bf16[2,2,288,2304]{3,2,1,0:T(8,128)(2,1)} %pad_maximum_fusion), calls=%async_computation.6 | async-start | bytes 10616832 | tf_op jit(solution)/shard_map/all_to_all | solution.py:87
  325.3 32.0 %all-to-all-start.5 = ((bf16[2,512,1152]{2,1,0:T(8,128)(2,1)}), bf16[2,512,1152]{2,1,0:T(8,128)(2,1)}, u32[]{:S(2)}, u32[]{:S(2)}) async-start(bf16[2,512,1152]{2,1,0:T(8,128)(2,1)} %broadcast_in_dim.41), calls=%async_computation.5 | async-start | bytes 4718592 | tf_op jit(solution)/shard_map/all_to_all | solution.py:14
  357.3 2.5 copy-start.2
  372.2 37.4 %all-to-all-start.8 = ((bf16[32,8,2304]{2,1,0:T(8,128)(2,1)}), bf16[32,8,2304]{2,1,0:T(8,128)(2,1)}, u32[]{:S(2)}, u32[]{:S(2)}) async-start(bf16[32,8,2304]{2,1,0:T(8,128)(2,1)} %reduce_sum.135), calls=%async_computation.8 | async-start | bytes 2359296 | tf_op jit(solution)/shard_map/all_to_all | solution.py:55
  411.1 0.6 copy-start.3
  430.0 22.3 %all-to-all-start.11 = ((bf16[32,8,2304]{2,1,0:T(8,128)(2,1)}), bf16[32,8,2304]{2,1,0:T(8,128)(2,1)}, u32[]{:S(2)}, u32[]{:S(2)}) async-start(bf16[32,8,2304]{2,1,0:T(8,128)(2,1)} %broadcast_in_dim.44), calls=%async_computation.11 | async-start | bytes 2359296 | tf_op jit(solution)/shard_map/all_to_all | solution.py:14
  459.3 1.8 copy-start
  495.6 1.8 copy-start.1
  506.1 30.9 %copy-start.4 = (bf16[8,2304]{1,0:T(8,128)(2,1)S(1)}, bf16[8,2304]{1,0:T(8,128)(2,1)}, u32[]{:S(2)}) copy-start(bf16[8,2304]{1,0:T(8,128)(2,1)} %get-tuple-element.10) | copy-start | bytes 110596
